TPU v7x, 32 devices: a whole 2x2x4 slice. The times are simulated.
32 devices in a mesh: tp: 4 (over z), dp: 8 (over y, x, core).
Axes of the slice: x: 2, y: 2, z: 4, core: 2. Of those that a mesh axis runs over, the one named last changes fastest.
Arguments:
- a_mat: bfloat16 [5120, 32768], P(('dp', 'tp'))
- b_mat: bfloat16 [32768, 13824], P(('dp', 'tp'))
Outputs:
- output: bfloat16 [5120, 13824], P(('dp', 'tp'))
All inputs are finite; a program needn't handle non-finite values.
Results may differ from a plain program's by a relative error of at most 0.001.
Values are sent between devices in bfloat16 or wider.
A program may use at most 1 GiB of HBM per device.

v0:
```python
import jax
import jax.numpy as jnp
from jax import lax
from jax.sharding import PartitionSpec as P


def solution(mesh):
    spec_rows = P(("dp", "tp"), None)

    def local_block(a_rows, b_rows):
        a_cols = lax.all_to_all(a_rows, "dp", 1, 0, tiled=True)
        b_slab = lax.all_gather(b_rows, "tp", axis=0, tiled=True)
        part_prod = jnp.dot(a_cols, b_slab, preferred_element_type=jnp.float32)
        summed = lax.psum_scatter(part_prod, "dp", scatter_dimension=0, tiled=True)
        return summed.astype(jnp.bfloat16)

    return jax.shard_map(local_block, mesh=mesh, in_specs=(spec_rows, spec_rows), out_specs=spec_rows, check_vma=False)
```

profile of v0, /device:TPU:0, one launch (start us, length us, event | category | flops | bytes accessed | tf_op | source)
XLA Modules:
  0.0 2450.4 jit_solution(87497554554055384)
XLA Ops:
  6.5 0.0 all-gather.2.cloned.1.call-start
  6.5 0.7 all-gather.2.cloned.1.call-update
  7.3 0.0 reduce-scatter.2.cloned.1.call-start
  7.3 9.4 copy.7
  16.7 123.0 %all_to_all.19 = bf16[160,8,4096]{2,0,1:T(8,128)(2,1)} all-to-all(bf16[160,8,4096]{2,0,1:T(8,128)(2,1)} %bitcast.9), channel_id=1, replica_groups=mesh['tp'=4,'dp'=8] {'dp'}, dimensions={1} | all-to-all | bytes 20971520 | tf_op jit(solution)/shard_map/all_to_all | solution.py:11
  139.8 1739.5 %all-gather.2.cloned.1.call-done = bf16[4096,13824]{1,0:T(8,128)(2,1)} async-done(((bf16[1024,13824]{1,0:T(8,128)(2,1)}), bf16[4096,13824]{1,0:T(8,128)(2,1)}) %all-gather.2.cloned.1.call-update) | async-done | bytes 113246224 | tf_op jit(solution)/shard_map/all_gather | solution.py:12
  1879.3 159.1 %fusion = f32[1280,13824]{1,0:T(8,128)} fusion(bf16[1280,4096]{1,0:T(8,128)(2,1)} %bitcast.11, bf16[4096,13824]{1,0:T(8,128)(2,1)} %all-gather.2.cloned.1.call-done), kind=kOutput, calls=%fused_computation.1 | convolution fusion | flops 144955146240 | bytes 194510848 | tf_op jit(solution)/shard_map/dot_general | solution.py:13
  2038.3 0.0 reduce-scatter.2.cloned.1.call-update
  2038.3 399.2 %reduce-scatter.2.cloned.1.call-done = f32[160,13824]{1,0:T(8,128)} async-done(((f32[1280,13824]{1,0:T(8,128)}), f32[160,13824]{1,0:T(8,128)}) %reduce-scatter.2.cloned.1.call-update) | async-done | bytes 8847376 | tf_op jit(solution)/shard_map/reduce_scatter | solution.py:14
  2437.5 6.0 convert_element_type.3
Async XLA Ops:
  6.5 1872.7 %all-gather.2.cloned.1.call-start = ((), (), s32[]{:S(2)}) async-start(), calls=%async_computation.2 | async-start | bytes 141557760 | tf_op jit(solution)/shard_map/all_gather | solution.py:12
  7.3 2430.3 %reduce-scatter.2.cloned.1.call-start = ((), (), s32[]{:S(2)}) async-start(), calls=%async_computation.3 | async-start | bytes 79626240 | tf_op jit(solution)/shard_map/reduce_scatter | solution.py:14
Sparse Core Ops, SparseCore 0:
  8.9 1870.2 all-gather.1
  2038.5 399.0 reduce-scatter.1
where the time goes:
time: 2450 us
  waiting for transfers between devices  2140 us (87%)
  matrix products  159 us (6%)
  blocking collectives  123 us (5%)
    all_gather x1, waiting for transfers between devices, local_block(): b_slab = lax.all_gather(b_rows, 'tp', axis=0, tiled=True)  1740 us
    reduce_scatter x1, waiting for transfers between devices, local_block(): summed = lax.psum_scatter(part_prod, 'dp', scatter_dimension=0, tiled=True)  399 us
    dot_general x1, matrix products, local_block(): part_prod = jnp.dot(a_cols, b_slab, preferred_element_type=jnp.float32)  159 us
    all_to_all x1, blocking collectives, local_block(): a_cols = lax.all_to_all(a_rows, 'dp', 1, 0, tiled=True)  123 us
  transfers between devices with their start and end apart: 2, of which 2 were waited for; matrix products, arithmetic and copies ran while one was open for 0% of the time, Pallas kernels for 0%

commit v1 on v0

v1 whole, which is shorter than its diff:
```python
import functools

import jax
import jax.numpy as jnp
from jax import lax
from jax.experimental import pallas as pl
from jax.experimental.pallas import tpu as pltpu
from jax.sharding import PartitionSpec as P

TILE = 384
LAG = 6
B_SEND, B_PASS, B_HAVE, A_SEND, A_PASS, A_HAVE, MULT, SUM = range(8)

ROW_ORDER = ((1, 2, 3, 0), (2, 3, 0, 1), (1, 0, 3, 2), (2, 1, 0, 3))
A_DEST = ((1, 3, 2), (0, 3, 2), (3, 0, 1), (2, 0, 1))


def make_steps(tiles):
    arrivals = ["B", "B", "A", "B", "A", "B", "B", "A"] + ["B"] * (tiles - 5) + ["A"]
    seq = [(what, arrivals[:n].count(what)) for n, what in enumerate(arrivals)]
    steps, sums = [], []
    have_a, have_b = [], []
    last = [None, None]

    def comm(op_b, op_a, item):
        steps.append((op_b, 0, item[1], 0, 0) if item[0] == "B" else (op_a, item[1], 0, 0, 0))

    def mult(u, j):
        steps.append((MULT, u, j, int(last[0] != u), int(last[1] != j)))
        last[0], last[1] = u, j

    done = 0
    comm(B_SEND, A_SEND, seq[0])
    for n, item in enumerate(seq):
        comm(B_PASS, A_PASS, item)
        if n + 1 < len(seq):
            comm(B_SEND, A_SEND, seq[n + 1])
        comm(B_HAVE, A_HAVE, item)
        if item[0] == "B":
            have_b.append(item[1])
            for u in (2, 1, 0):
                if u in have_a:
                    mult(u, item[1])
            sums += [(u, item[1]) for u in (1, 0, 2) if u in have_a]
        else:
            have_a.append(item[1])
            for j in have_b:
                mult(item[1], j)
            sums += [(item[1], j) for j in have_b]
        while done < len(sums) - LAG and sums[done][0] < 3:
            steps.append((SUM, *sums[done], 0, 0))
            done += 1
    rest = [s for s in sums[done:] if s[0] < 3]
    for j in range(tiles):
        now = [s for s in rest if s[1] == j]
        steps += [(SUM, *s, 0, 0) for s in [*now, (3, j)]]
    return steps


def choose(index, values):
    out = jnp.int32(values[-1])
    for k in range(len(values) - 2, -1, -1):
        if values[k] != values[k + 1] or k == 0:
            out = jnp.where(index <= k, jnp.int32(values[k]), out)
    return out


def kernel(
    steps, a, b, c_out, a_all, b_all, part, low, high,
    av, bv, acc, s0, s1, s2, cv,
    a1_s, a1_r, ax_s, ax_r, ay_s, ay_r, fx_s, fx_r, fy_s, fy_r,
    b_s, b_r, own_s, own_r, pass_s, pass_r, up_s, low_r, high_r, fin_s, fin_r, fin_l, lda, ldb, st, ls,
):
    rows, depth = a.shape[0], b.shape[0]
    tile = part.shape[3]
    tiles = part.shape[1]
    wide = tile * tiles
    half = rows // 2
    z, d = lax.axis_index("tp"), lax.axis_index("dp")
    q = d // 2
    core, x, y = d % 2, q % 2, d // 4
    q_x, q_y = q + 1 - 2 * x, q + 2 - 4 * y
    q_d = q_x + 2 - 4 * y
    peers = (q_x, q_y, q_d)

    def at(plane, chip):
        return {"tp": plane, "dp": chip * 2 + core}

    sibling = {"tp": z, "dp": d + 1 - 2 * core}

    def remote(src, dst, send, recv, to):
        return pltpu.make_async_remote_copy(
            src_ref=src, dst_ref=dst, send_sem=send, recv_sem=recv, device_id=to, device_id_type=pl.DeviceIdType.MESH
        )

    def row_group(u):
        return choose(z * 4 + u, [i for order in ROW_ORDER for i in order])

    def a_rows(i, chip, first=0, count=rows):
        return a_all.at[i, pl.ds(pl.multiple_of(chip * rows + first, half), count), :]

    def b_rows(j, dev):
        return b_all.at[j, pl.ds(pl.multiple_of(dev * depth, depth), depth), :]

    def columns(chip, j):
        return pl.ds(pl.multiple_of(chip * wide + j * tile, tile), tile)

    def k_block(dev, plane):
        return pl.ds(pl.multiple_of((dev * 4 + plane) * depth, depth), depth)

    barrier = pltpu.get_barrier_semaphore()
    for plane in range(1, 4):
        pl.semaphore_signal(barrier, inc=1, device_id=at((z + plane) % 4, q), device_id_type=pl.DeviceIdType.MESH)
    for chip in peers:
        pl.semaphore_signal(barrier, inc=1, device_id=at(z, chip), device_id_type=pl.DeviceIdType.MESH)
    pl.semaphore_signal(barrier, inc=1, device_id=sibling, device_id_type=pl.DeviceIdType.MESH)
    pl.semaphore_wait(barrier, 7)

    def a1(m, dev):
        plane = choose(z * 3 + m, [p for dest in A_DEST for p in dest])
        return remote(
            a.at[:, k_block(dev, plane)],
            a_all.at[z, pl.ds(pl.multiple_of(q * rows, half), rows), pl.ds(pl.multiple_of(dev * depth, depth), depth)],
            a1_s.at[m], a1_r.at[z], at(plane, q),
        )

    for m in range(3):

        @pl.loop(0, 8)
        def _(dev):
            a1(m, dev).start()

    own_in = [pltpu.make_async_copy(a.at[:, k_block(dev, z)], av.at[dev, pl.ds(0, rows), :], lda.at[dev]) for dev in range(8)]
    own_out = [
        pltpu.make_async_copy(
            av.at[dev, pl.ds(0, rows), :],
            a_all.at[z, pl.ds(pl.multiple_of(q * rows, half), rows), pl.ds(dev * depth, depth)],
            ldb.at[dev],
        )
        for dev in range(8)
    ]
    for copy in own_in:
        copy.start()
    for copy, put in zip(own_in, own_out, strict=True):
        copy.wait()
        put.start()
    for put in own_out:
        put.wait()

    def b_copy(j, n):
        return remote(b.at[:, columns(peers[n], j)], b_rows(j, d), b_s.at[j, n], b_r.at[j, n], at(z, peers[n]))

    def b_landed(j, n):
        dst = b_rows(j, peers[n] * 2 + core)
        return remote(dst, dst, b_s.at[j, n], b_r.at[j, n], at(z, peers[n]))

    def b_own(j):
        return remote(b.at[:, columns(q, j)], b_rows(j, d), own_s.at[j], own_r.at[j], sibling)

    def b_pass(j, n):
        dst = b_rows(j, peers[n] * 2 + core)
        return remote(dst, dst, pass_s.at[j, n], pass_r.at[j, n], sibling)

    def b_passed(j, n):
        dst = b_rows(j, peers[n] * 2 + 1 - core)
        return remote(dst, dst, pass_s.at[j, n], pass_r.at[j, n], sibling)

    def b_own_passed(j):
        dst = b_rows(j, d + 1 - 2 * core)
        return remote(dst, dst, own_s.at[j], own_r.at[j], sibling)

    def a_x(u, i, chip):
        return remote(a_rows(i, chip), a_rows(i, chip), ax_s.at[u], ax_r.at[u], at(z, q_x))

    def a_y(u, i, chip):
        return remote(a_rows(i, chip), a_rows(i, chip), ay_s.at[u], ay_r.at[u], at(z, q_y))

    def f_y(u, i, chip):
        return remote(a_rows(i, chip, 0, half), a_rows(i, chip, 0, half), fy_s.at[u], fy_r.at[u], at(z, q_y))

    def f_x(u, i, chip):
        return remote(a_rows(i, chip, half, half), a_rows(i, chip, half, half), fx_s.at[u], fx_r.at[u], at(z, q_x))

    def up(i, j):
        return remote(part.at[i, j], low.at[i, j], up_s.at[i, j], low_r.at[i, j], at(jnp.minimum(z + 1, 3), q))

    def down(i, j):
        return remote(part.at[i, j], high.at[i, j], up_s.at[i, j], high_r.at[i, j], at(jnp.maximum(z - 1, 0), q))

    def send_part(i, j):
        @pl.when(i > z)
        def _():
            up(i, j).start()

        @pl.when(i < z)
        def _():
            down(i, j).start()

    def final(j, n):
        return remote(
            cv.at[j % 2, pl.ds(pl.multiple_of(peers[n] * rows, half), rows), :],
            c_out.at[:, columns(q, j)],
            fin_s.at[j, n], fin_r.at[j, n], at(z, peers[n]),
        )

    def final_landed(j, n):
        dst = c_out.at[:, columns(peers[n], j)]
        return remote(cv.at[j % 2, pl.ds(0, rows), :], dst, fin_s.at[j, n], fin_r.at[j, n], at(z, peers[n]))

    def final_own(j):
        return pltpu.make_async_copy(
            cv.at[j % 2, pl.ds(pl.multiple_of(q * rows, half), rows), :], c_out.at[:, columns(q, j)], fin_l.at[j % 2]
        )

    def load_a(i, k):
        dev = (d + k) % 8
        return pltpu.make_async_copy(a_all.at[i, :, pl.ds(pl.multiple_of(dev * depth, depth), depth)], av.at[k], lda.at[k])

    def load_b(j, k):
        return pltpu.make_async_copy(b_rows(j, (d + k) % 8), bv.at[k], ldb.at[k])

    def load_b_own(j):
        return pltpu.make_async_copy(b.at[:, columns(q, j)], bv.at[0], ldb.at[0])

    def multiply(u, j, new_a, new_b):
        i = row_group(u)

        @pl.when(new_b == 1)
        def _():
            load_b_own(j).start()

        @pl.when(new_a == 1)
        def _():
            load_a(i, 0).start()

        @pl.loop(1, 8)
        def _(k):
            @pl.when(new_b == 1)
            def _():
                load_b(j, k).start()

            @pl.when(new_a == 1)
            def _():
                load_a(i, k).start()

        acc[...] = jnp.zeros_like(acc)

        @pl.loop(0, 8)
        def _(k):
            @pl.when(new_a == 1)
            def _():
                load_a(i, k).wait()

            @pl.when(new_b == 1)
            def _():
                load_b(j, k).wait()

            acc[...] += jnp.dot(av[k], bv[k], preferred_element_type=jnp.float32)

        put = pltpu.make_async_copy(acc, part.at[i, j], st)
        put.start()
        put.wait()

        @pl.when(((z == 0) | (z == 3)) & (i != z))
        def _():
            send_part(i, j)

    def add_up(u, j):
        i = row_group(u)
        has_low = (z > 0) & (z <= i)
        has_high = (z < 3) & (z >= i)

        @pl.when((z == 1) | (z == 2) | (u == 3))
        def _():
            mine = pltpu.make_async_copy(part.at[i, j], s0, ls.at[0])
            below = pltpu.make_async_copy(low.at[i, j], s1, ls.at[1])
            above = pltpu.make_async_copy(high.at[i, j], s2, ls.at[2])
            mine.start()

            @pl.when(has_low)
            def _():
                up(i, j).wait_recv()
                below.start()

            @pl.when(has_high)
            def _():
                down(i, j).wait_recv()
                above.start()

            mine.wait()

            @pl.when(has_low)
            def _():
                below.wait()
                s0[...] += s1[...]

            @pl.when(has_high)
            def _():
                above.wait()
                s0[...] += s2[...]

            @pl.when(i == z)
            def _():
                @pl.when(j >= 2)
                def _():
                    for n in range(3):
                        final(j - 2, n).wait_send()
                    final_own(j - 2).wait()

                cv[j % 2] = s0[...].astype(cv.dtype)
                for n in range(3):
                    final(j, n).start()
                final_own(j).start()

            @pl.when(i != z)
            def _():
                put = pltpu.make_async_copy(s0, part.at[i, j], st)
                put.start()
                put.wait()
                send_part(i, j)

    codes = [op | u << 3 | j << 5 | new_a << 10 | new_b << 11 for op, u, j, new_a, new_b in steps]

    @pl.loop(0, len(steps))
    def _(t):
        code = choose(t, codes)
        op, u, j, new_a, new_b = code % 8, code // 8 % 4, code // 32 % 32, code // 1024 % 2, code // 2048
        i = row_group(u)

        @pl.when(op == B_SEND)
        def _():
            for n in range(3):
                b_copy(j, n).start()
            b_own(j).start()

        @pl.when(op == B_PASS)
        def _():
            for n in range(3):
                b_landed(j, n).wait_recv()
                b_pass(j, n).start()

        @pl.when(op == B_HAVE)
        def _():
            b_own_passed(j).wait_recv()
            for n in range(3):
                b_passed(j, n).wait_recv()

        @pl.when(op == A_SEND)
        def _():
            @pl.when(i != z)
            def _():
                landed = a_rows(i, q)
                remote(landed, landed, a1_s.at[0], a1_r.at[i], at(z, q_x)).wait_recv()

            a_x(u, i, q).start()
            a_y(u, i, q).start()

        @pl.when(op == A_PASS)
        def _():
            a_x(u, i, q_x).wait_recv()
            f_y(u, i, q_x).start()
            a_y(u, i, q_y).wait_recv()
            f_x(u, i, q_y).start()

        @pl.when(op == A_HAVE)
        def _():
            f_y(u, i, q_d).wait_recv()
            f_x(u, i, q_d).wait_recv()

        @pl.when(op == MULT)
        def _():
            multiply(u, j, new_a, new_b)

        @pl.when(op == SUM)
        def _():
            add_up(u, j)

    for m in range(3):
        remote(a_rows(z, q), a_rows(z, q), a1_s.at[m], a1_r.at[z], at(z, q_x)).wait_send()

    @pl.loop(0, 4)
    def _(u):
        i = row_group(u)
        a_x(u, i, q).wait_send()
        a_y(u, i, q).wait_send()
        f_y(u, i, q_x).wait_send()
        f_x(u, i, q_y).wait_send()

    @pl.loop(0, tiles)
    def _(j):
        for n in range(3):
            b_copy(j, n).wait_send()
            b_pass(j, n).wait_send()
        b_own(j).wait_send()

        @pl.loop(0, 3)
        def _(u):
            up(row_group(u), j).wait_send()

        for n in range(3):
            final_landed(j, n).wait_recv()

    @pl.loop(tiles - 2, tiles)
    def _(j):
        for n in range(3):
            final(j, n).wait_send()
        final_own(j).wait()


def solution(mesh):
    spec_rows = P(("dp", "tp"), None)

    def local_block(a, b):
        rows, depth, cols = a.shape[0], b.shape[0], b.shape[1]
        wide = cols // 4
        tile = min(TILE, wide // 9)
        tiles = wide // tile
        group = 4 * rows
        steps = make_steps(tiles)
        dma = pltpu.SemaphoreType.DMA
        any_space = pl.BlockSpec(memory_space=pl.ANY)
        out = pl.pallas_call(
            functools.partial(kernel, steps),
            out_shape=[
                jax.ShapeDtypeStruct((rows, cols), jnp.bfloat16),
                jax.ShapeDtypeStruct((4, group, 8 * depth), jnp.bfloat16),
                jax.ShapeDtypeStruct((tiles, 8 * depth, tile), jnp.bfloat16),
                jax.ShapeDtypeStruct((4, tiles, group, tile), jnp.float32),
                jax.ShapeDtypeStruct((4, tiles, group, tile), jnp.float32),
                jax.ShapeDtypeStruct((4, tiles, group, tile), jnp.float32),
            ],
            in_specs=[any_space] * 2,
            out_specs=[any_space] * 6,
            scratch_shapes=[
                pltpu.VMEM((8, group, depth), jnp.bfloat16),
                pltpu.VMEM((8, depth, tile), jnp.bfloat16),
                pltpu.VMEM((group, tile), jnp.float32),
                pltpu.VMEM((group, tile), jnp.float32),
                pltpu.VMEM((group, tile), jnp.float32),
                pltpu.VMEM((group, tile), jnp.float32),
                pltpu.VMEM((2, group, tile), jnp.bfloat16),
                dma((3,)), dma((4,)),
                dma((4,)), dma((4,)), dma((4,)), dma((4,)),
                dma((4,)), dma((4,)), dma((4,)), dma((4,)),
                dma((tiles, 3)), dma((tiles, 3)), dma((tiles,)), dma((tiles,)), dma((tiles, 3)), dma((tiles, 3)),
                dma((4, tiles)), dma((4, tiles)), dma((4, tiles)),
                dma((tiles, 3)), dma((tiles, 3)), dma((2,)),
                dma((8,)), dma((8,)), dma, dma((3,)),
            ],
            compiler_params=pltpu.CompilerParams(
                collective_id=0, has_side_effects=True, vmem_limit_bytes=60 * 1024 * 1024
            ),
        )(a, b)
        return out[0]

    return jax.shard_map(local_block, mesh=mesh, in_specs=(spec_rows, spec_rows), out_specs=spec_rows, check_vma=False)
```

time: 2450 us -> 1100 us (0.45)
  the two profiles are of different devices: /device:TPU:0 before, /device:TPU:11 now
where the time goes in v1:
time: 1100 us
  Pallas kernels  1100 us (100%)
    pallas_call x1, Pallas kernels, local_block(): pl.pallas_call(functools.partial(kernel, steps), out_shape=[jax.ShapeDtyp...  1100 us

profile of v1, /device:TPU:11, one launch (start us, length us, event | category | flops | bytes accessed | tf_op | source)
XLA Modules:
  0.0 1099.7 jit_solution(6130266809415927534)
XLA Ops:
  0.0 1095.1 %shard_map.28 = (bf16[160,13824]{1,0:T(8,128)(2,1)}, bf16[4,640,8192]{2,1,0:T(8,128)(2,1)}, bf16[9,8192,384]{2,1,0:T(8,128)(2,1)}, f32[4,9,640,384]{3,2,1,0:T(8,...) custom-call(bf16[160,32768]{1,0:T(8,128)(2,1)} %a.1, bf16[1024,13824]{1,0:T(8,128)(2,1)} %b.1), custom_call_target="tpu_custom_call" | custom-call | tf_op jit(solution)/shard_map/pallas_call | solution.py:422
  1095.1 4.6 copy.4
